TPU v7x, 32 devices: a whole 2x2x4 slice. The times are simulated.
32 devices in a mesh: dp: 8 (over y, x, core), enc: 4 (over z).
Axes of the slice: x: 2, y: 2, z: 4, core: 2. Of those that a mesh axis runs over, the one named last changes fastest.
Arguments:
- patches: bfloat16 [4096, 1280], P(('dp', 'enc')), may hold values from -6 to 6
- cotangent: bfloat16 [4096, 1280], P(('dp', 'enc')), may hold values from -6 to 6
- counts: int32 [8, 4, 8, 4], replicated, may hold values from 0 to 8, as said below
- gain: float32 [1280], replicated, may hold values from 0.25 to 1.75
- w_qkv: bfloat16 [1280, 3840], replicated, may hold values from -0.15625 to 0.15625
- w_out: bfloat16 [1280, 1280], replicated, may hold values from -0.15625 to 0.15625
Outputs:
- output: bfloat16 [4096, 1280], P(('dp', 'enc'))
- grad_patches: bfloat16 [4096, 1280], P(('dp', 'enc'))
Inputs may be any that keep to these rules, and one draw needn't show every extreme that they name: For every sending device the counts to all destinations sum to 128; each count is at most 8; some destination device receives 8 rows from every sender, and every sender fills its 8 slots to some destination.
All inputs are finite; a program needn't handle non-finite values.
Results may differ from a plain program's by a relative error of at most 0.0039.
Values may be sent and summed in bfloat16 or wider, within the bound.
No kernel may reach another device: no remote copies, remote signals or barrier semaphores. Data moves between devices by JAX's collectives and lax.ppermute only.
A program may use at most 128 MiB of HBM per device.

v0:
```python
import jax
import jax.numpy as jnp
from jax import lax
from jax.sharding import PartitionSpec as P

H = 16
HD = 80


eps = 1e-06


def send_home(values, plan_row, offsets, cap):
    home = values.shape[0]
    devices = plan_row.shape[0]
    ends = offsets + plan_row
    positions = jnp.arange(home, dtype=jnp.int32)
    target = jnp.sum((ends[None, :] <= positions[:, None]).astype(jnp.int32), axis=1)
    onehot = (jnp.arange(devices, dtype=jnp.int32)[None, :] == target[:, None]).astype(jnp.int32)
    begin = jnp.sum(onehot * offsets[None, :], axis=1)
    return target * cap + positions - begin


def shards(patches, cotangent, counts, gain, w_qkv, w_out):
    home, width = patches.shape
    dp_count = lax.axis_size("dp")
    enc_count = lax.axis_size("enc")
    devices = dp_count * enc_count
    cap = 2 * home // devices
    rows = devices * cap
    inv_scale = HD ** (-0.5)
    group = lax.axis_index("dp")
    member = lax.axis_index("enc")
    plan = counts.reshape(devices, devices)
    plan_row = lax.dynamic_index_in_dim(plan, group * enc_count + member, 0, keepdims=False)
    offsets = jnp.cumsum(plan_row) - plan_row
    slots = jnp.arange(cap, dtype=jnp.int32)
    filled = (slots[None, :] < plan_row[:, None]).reshape(-1, 1)
    take = jnp.clip(offsets[:, None] + slots[None, :], 0, home - 1).reshape(-1)
    packed_x = jnp.where(filled, patches[take], 0)
    packed_dy = jnp.where(filled, cotangent[take], 0)
    arrived_x, arrived_dy = (
        lax.all_to_all(packed_x, ("dp", "enc"), split_axis=0, concat_axis=0, tiled=True),
        lax.all_to_all(packed_dy, ("dp", "enc"), split_axis=0, concat_axis=0, tiled=True),
    )
    incoming = lax.dynamic_index_in_dim(counts, group, 2, keepdims=False)
    arrivals = jnp.transpose(incoming, (2, 0, 1)).reshape(enc_count, devices)
    key_valid = (slots[None, None, :] < arrivals[:, :, None]).reshape(1, -1)
    xf = arrived_x.astype(jnp.float32)
    inv = lax.rsqrt(jnp.mean(xf * xf, axis=-1, keepdims=True) + eps)
    normed = (xf * inv * gain).astype(jnp.bfloat16)
    query = jnp.dot(normed, w_qkv[:, :width], preferred_element_type=jnp.float32).astype(
        jnp.bfloat16
    )
    all_normed = lax.all_gather(normed, "enc", axis=0, tiled=True)
    all_kv = jnp.dot(all_normed, w_qkv[:, width:], preferred_element_type=jnp.float32).astype(
        jnp.bfloat16
    )
    total = all_kv.shape[0]
    d_context = lax.dot_general(
        arrived_dy, w_out, (((1,), (1,)), ((), ())), preferred_element_type=jnp.float32
    ).astype(jnp.bfloat16)
    query_heads = jnp.transpose(query.reshape(rows, H, HD), (1, 0, 2))
    key_heads = jnp.transpose(all_kv[:, :width].reshape(total, H, HD), (1, 0, 2))
    value_heads = jnp.transpose(all_kv[:, width:].reshape(total, H, HD), (1, 0, 2))
    dctx_heads = jnp.transpose(d_context.reshape(rows, H, HD), (1, 0, 2))

    def one_head(operands):
        query_h, key_h, value_h, dctx_h = operands
        scores = (
            lax.dot_general(
                query_h, key_h, (((1,), (1,)), ((), ())), preferred_element_type=jnp.float32
            )
            * inv_scale
        )
        scores = jnp.where(key_valid, scores, -1000000000.0)
        attn = jax.nn.softmax(scores, axis=-1)
        attn_b = attn.astype(jnp.bfloat16)
        context_h = jnp.dot(attn_b, value_h, preferred_element_type=jnp.float32).astype(
            jnp.bfloat16
        )
        d_attn = lax.dot_general(
            dctx_h, value_h, (((1,), (1,)), ((), ())), preferred_element_type=jnp.float32
        )
        inner = jnp.sum(attn * d_attn, axis=-1, keepdims=True)
        d_scores_b = (attn * (d_attn - inner)).astype(jnp.bfloat16)
        d_query_h = jnp.dot(d_scores_b, key_h, preferred_element_type=jnp.float32) * inv_scale
        d_key_h = (
            lax.dot_general(
                d_scores_b, query_h, (((0,), (0,)), ((), ())), preferred_element_type=jnp.float32
            )
            * inv_scale
        )
        d_value_h = lax.dot_general(
            attn_b, dctx_h, (((0,), (0,)), ((), ())), preferred_element_type=jnp.float32
        )
        return (context_h, d_query_h, d_key_h, d_value_h)

    context_all, dq_all, dk_all, dv_all = lax.map(
        one_head, (query_heads, key_heads, value_heads, dctx_heads)
    )
    context = jnp.transpose(context_all, (1, 0, 2)).reshape(rows, width)
    output = (xf + jnp.dot(context, w_out, preferred_element_type=jnp.float32)).astype(jnp.bfloat16)
    back_out = lax.all_to_all(output, ("dp", "enc"), split_axis=0, concat_axis=0, tiled=True)
    d_query = jnp.transpose(dq_all, (1, 0, 2)).reshape(rows, width)
    d_kv = jnp.concatenate(
        [
            jnp.transpose(dk_all, (1, 0, 2)).reshape(total, width),
            jnp.transpose(dv_all, (1, 0, 2)).reshape(total, width),
        ],
        axis=-1,
    )
    summed_kv = lax.psum_scatter(
        d_kv.astype(jnp.bfloat16), "enc", scatter_dimension=0, tiled=True
    ).astype(jnp.float32)
    d_proj = jnp.concatenate([d_query, summed_kv], axis=-1).astype(jnp.bfloat16)
    d_normed = lax.dot_general(
        d_proj, w_qkv, (((1,), (1,)), ((), ())), preferred_element_type=jnp.float32
    )
    scaled = gain * d_normed
    grad = (
        arrived_dy.astype(jnp.float32)
        + inv * scaled
        - xf * inv**3 * jnp.mean(xf * scaled, axis=-1, keepdims=True)
    )
    grad = grad.astype(jnp.bfloat16)
    back_grad = lax.all_to_all(grad, ("dp", "enc"), split_axis=0, concat_axis=0, tiled=True)
    picked = send_home(patches, plan_row, offsets, cap)
    result_out = back_out[picked]
    result_grad = back_grad[picked]
    return (result_out, result_grad)


def solution(mesh):
    return jax.shard_map(
        shards,
        mesh=mesh,
        in_specs=(P(("dp", "enc"), None), P(("dp", "enc"), None), P(), P(), P(), P()),
        out_specs=(P(("dp", "enc"), None), P(("dp", "enc"), None)),
        check_vma=False,
    )
```

profile of v0, /device:TPU:1, one launch (start us, length us, event | category | flops | bytes accessed | tf_op | source)
XLA Modules:
  0.0 460.2 jit_solution(6276375779573839618)
XLA Ops:
  9.2 3.6 gather_fusion.1
  12.8 3.6 gather_fusion
  16.4 2.3 bitcast_select_fusion
  18.7 24.9 %all_to_all.39 = bf16[32,8,1280]{2,1,0:T(8,128)(2,1)S(1)} all-to-all(bf16[32,8,1280]{2,1,0:T(8,128)(2,1)S(1)} %get-tuple-element.131), channel_id=1, replica_groups=mesh['dp'=8,'enc'=4] {'dp','enc'}, dimensions={0} | all-to-all | bytes 1310720 | tf_op jit(solution)/shard_map/all_to_all | solution.py:43
  44.9 2.2 fusion.58
  47.0 3.2 all-to-all-start.1
  51.0 4.2 fusion.46
  55.2 2.2 copy.30
  57.4 24.9 %all-to-all-done.1 = bf16[32,8,1280]{2,1,0:T(8,128)(2,1)} async-done(((bf16[32,8,1280]{2,1,0:T(8,128)(2,1)}), bf16[32,8,1280]{2,1,0:T(8,128)(2,1)}, u32[]{:S(2)}, u32[]{:S(2)}) %all-to-all-start.1) | async-done | bytes 655392 | tf_op jit(solution)/shard_map/all_to_all | solution.py:44
  82.3 3.0 convolution_convert_fusion.1
  85.3 2.2 copy.33
  87.5 22.9 %all-gather.2.cloned.1.call-done = bf16[1024,1280]{1,0:T(8,128)(2,1)} async-done(((bf16[256,1280]{1,0:T(8,128)(2,1)}), bf16[1024,1280]{1,0:T(8,128)(2,1)}) %all-gather.2.cloned.1.call-update) | async-done | bytes 2621456 | tf_op jit(solution)/shard_map/all_gather | solution.py:55
  110.4 10.4 %fusion.41 = bf16[1024,2560]{1,0:T(8,128)(2,1)S(1)} fusion(bf16[1024,1280]{1,0:T(8,128)(2,1)} %all-gather.2.cloned.1.call-done, bf16[1280,3840]{1,0:T(8,128)(2,1)} %param.12), kind=kOutput, calls=%fused_computation.51 | convolution fusion | flops 6713507840 | bytes 14417920 | tf_op jit(solution)/shard_map/dot_general | solution.py:56
  120.8 2.6 fusion.70
  123.4 4.5 copy.32
  128.0 4.5 copy.31
  132.4 173.6 %while.17 = (s32[]{:T(128)}, bf16[16,256,80]{1,2,0:T(8,128)(2,1)}, bf16[16,256,80]{1,2,0:T(8,128)(2,1)}, bf16[16,1024,80]{1,2,0:T(8,128)(2,1)}, bf16[16,1024,80]...) while((s32[]{:T(128)}, bf16[16,256,80]{1,2,0:T(8,128)(2,1)}, ...), condition=%wide.region_6.7_spmd.clone, body=%wide.region_2.6_spmd.clone.sunk | while | flops 257024256 | bytes 11583093 | solution.py:99
  145.1 1.9 fusion.105
  177.7 1.9 fusion.105
  188.6 1.9 fusion.105
  232.0 1.9 fusion.105
  275.4 1.9 fusion.105
  306.1 5.4 %pad_maximum_fusion = bf16[1024,2560]{0,1:T(8,128)(2,1)} fusion(bf16[1024,1280]{0,1:T(8,128)(2,1)} %bitcast.178, bf16[1024,1280]{0,1:T(8,128)(2,1)} %bitcast.179), kind=kLoop, calls=%fused_computation.52 | loop fusion | flops 10485760 | bytes 10485760 | tf_op jit(solution)/shard_map/concatenate | solution.py:106
  311.5 3.2 fusion.50
  314.7 3.9 all-to-all-start.2
  318.6 96.1 %reduce-scatter.2.cloned.1.call-done = bf16[256,2560]{0,1:T(8,128)(2,1)} async-done(((bf16[1024,2560]{0,1:T(8,128)(2,1)}), bf16[256,2560]{0,1:T(8,128)(2,1)}) %reduce-scatter.2.cloned.1.call-update) | async-done | bytes 1310736 | tf_op jit(solution)/shard_map/reduce_scatter | solution.py:113
  414.7 7.5 %fusion.62 = (f32[256]{0:T(256)S(1)}, f32[256,1280]{1,0:T(8,128)S(1)}) fusion(bf16[32,8,1280]{2,1,0:T(8,128)(2,1)} %copy-done.1, bf16[1280,3840]{1,0:T(8,128)(2,1)} %param.12, bf16[256,2560]{0,1:T(8,128)(2,1)} %reduce-scatter.2.cloned.1.call-done, bf16[256,1280]{0,1:T(8,128)(2,1)} %bitcast.185, f32[1280]{0:T(1024)S(1)} %copy-done.4), kind=kOutput, calls=%fused_computation.74 | convolution fusion | flops 2521825024 | bytes 13768704 | tf_op jit(solution)/shard_map/dot_general | solution.py:117
  422.2 2.3 fusion.64
  424.6 7.7 %all-to-all-start.3 = ((bf16[32,8,1280]{2,1,0:T(8,128)(2,1)}), bf16[32,8,1280]{2,1,0:T(8,128)(2,1)}, u32[]{:S(2)}, u32[]{:S(2)}) async-start(bf16[32,8,1280]{2,1,0:T(8,128)(2,1)} %fusion.64), calls=%async_computation.4 | async-start | bytes 1310720 | tf_op jit(solution)/shard_map/all_to_all | solution.py:127
  432.5 3.0 gather_fusion.2
  435.5 14.8 %all-to-all-done.3 = bf16[32,8,1280]{2,1,0:T(8,128)(2,1)} async-done(((bf16[32,8,1280]{2,1,0:T(8,128)(2,1)}), bf16[32,8,1280]{2,1,0:T(8,128)(2,1)}, u32[]{:S(2)}, u32[]{:S(2)}) %all-to-all-start.3) | async-done | bytes 655392 | tf_op jit(solution)/shard_map/all_to_all | solution.py:127
  450.4 3.0 gather_fusion.3
  (201 shorter events, 167.6 us)
Async XLA Ops:
  7.2 75.2 %copy-start = (bf16[1280,1280]{1,0:T(8,128)(2,1)S(1)}, bf16[1280,1280]{1,0:T(8,128)(2,1)}, u32[]{:S(2)}) copy-start(bf16[1280,1280]{1,0:T(8,128)(2,1)} %param.13) | copy-start | bytes 9830404
  7.2 103.2 %all-gather.2.cloned.1.call-start = ((), (), s32[]{:S(2)}) async-start(), calls=%async_computation.5 | async-start | bytes 3276800 | tf_op jit(solution)/shard_map/all_gather | solution.py:55
  16.4 28.4 %copy-start.4 = (f32[1280]{0:T(1024)S(1)}, f32[1280]{0:T(1024)}, u32[]{:S(2)}) copy-start(f32[1280]{0:T(1024)} %param.11) | copy-start | bytes 15364
  18.7 31.8 %copy-start.3 = (s32[8,4,8,4]{2,3,1,0:T(4,128)S(1)}, s32[8,4,8,4]{2,3,1,0:T(4,128)}, u32[]{:S(2)}) copy-start(s32[8,4,8,4]{2,3,1,0:T(4,128)} %param.10) | copy-start | bytes 12292
  43.7 0.9 copy-start.1
  47.0 35.3 %all-to-all-start.1 = ((bf16[32,8,1280]{2,1,0:T(8,128)(2,1)}), bf16[32,8,1280]{2,1,0:T(8,128)(2,1)}, u32[]{:S(2)}, u32[]{:S(2)}) async-start(bf16[32,8,1280]{2,1,0:T(8,128)(2,1)} %get-tuple-element.130), calls=%async_computation.1 | async-start | bytes 1310720 | tf_op jit(solution)/shard_map/all_to_all | solution.py:44
  50.3 364.5 %reduce-scatter.2.cloned.1.call-start = ((), (), s32[]{:S(2)}) async-start(), calls=%async_computation.6 | async-start | bytes 6553600 | tf_op jit(solution)/shard_map/reduce_scatter | solution.py:113
  314.7 109.9 %all-to-all-start.2 = ((bf16[32,8,1280]{2,1,0:T(8,128)(2,1)}), bf16[32,8,1280]{2,1,0:T(8,128)(2,1)}, u32[]{:S(2)}, u32[]{:S(2)}) async-start(bf16[32,8,1280]{2,1,0:T(8,128)(2,1)} %fusion.50), calls=%async_computation.2 | async-start | bytes 1310720 | tf_op jit(solution)/shard_map/all_to_all | solution.py:104
  414.7 7.5 %copy-start.2 = (bf16[32,8,1280]{2,1,0:T(8,128)(2,1)S(1)}, bf16[32,8,1280]{2,1,0:T(8,128)(2,1)}, u32[]{:S(2)}) copy-start(bf16[32,8,1280]{2,1,0:T(8,128)(2,1)} %copy-done.1) | copy-start | bytes 1966084
  424.6 25.8 %all-to-all-start.3 = ((bf16[32,8,1280]{2,1,0:T(8,128)(2,1)}), bf16[32,8,1280]{2,1,0:T(8,128)(2,1)}, u32[]{:S(2)}, u32[]{:S(2)}) async-start(bf16[32,8,1280]{2,1,0:T(8,128)(2,1)} %fusion.64), calls=%async_computation.4 | async-start | bytes 1310720 | tf_op jit(solution)/shard_map/all_to_all | solution.py:127
Sparse Core Ops, SparseCore 0:
  47.2 63.1 all-gather.1
  311.6 103.0 reduce-scatter.1
where the time goes:
time: 465 us; the launch traced here: 460 us
  matrix products  188 us (40%)
  waiting for transfers between devices  159 us (34%)
  local copies, waits for them, and re-layouts  34 us (7%)
  blocking collectives  24.9 us (5%)
  other arithmetic  24.6 us (5%)
  starting transfers between devices  15 us (3%)
  between operations  14.2 us (3%)
    reduce_scatter x1, waiting for transfers between devices, shards(): lax.psum_scatter(d_kv.astype(jnp.bfloat16), 'enc', scatter_dimension=0, t...  96.1 us
    dot_general x16, matrix products, one_head(): jnp.dot(attn_b, value_h, preferred_element_type=jnp.float32)  31 us
    dot_general x16, matrix products, one_head(): lax.dot_general(attn_b, dctx_h, (((0,), (0,)), ((), ())), preferred_eleme...  29.5 us
    dot_general x16, matrix products, one_head(): jnp.dot(d_scores_b, key_h, preferred_element_type=jnp.float32) * inv_scale  29.3 us
    dot_general x16, matrix products, one_head(): lax.dot_general(d_scores_b, query_h, (((0,), (0,)), ((), ())), preferred_...  26.5 us
    all_to_all x1, blocking collectives, shards(): lax.all_to_all(packed_x, ('dp', 'enc'), split_axis=0, concat_axis=0, tile...  24.9 us
    all_to_all x1, waiting for transfers between devices, shards(): lax.all_to_all(packed_dy, ('dp', 'enc'), split_axis=0, concat_axis=0, til...  24.9 us
    all_gather x1, waiting for transfers between devices, shards(): all_normed = lax.all_gather(normed, 'enc', axis=0, tiled=True)  22.9 us
  transfers between devices with their start and end apart: 5, of which 4 were waited for; matrix products, arithmetic and copies ran while one was open for 6% of the time, Pallas kernels for 0%

commit v1 on v0

v1 whole, which is shorter than its diff:
```python
import functools

import jax
import jax.numpy as jnp
from jax import lax
from jax.experimental import pallas as pl
from jax.experimental.pallas import tpu as pltpu
from jax.sharding import Mesh
from jax.sharding import PartitionSpec as P

H = 16
HD = 80
LANES = 128
eps = 1e-06
LOG2E = 1.4426950408889634
DEAD = -1000000000.0
VMEM_LIMIT = 56 * 1024 * 1024


def nt_dot(a, b):
    return lax.dot_general(a, b, (((1,), (1,)), ((), ())), preferred_element_type=jnp.float32)


def nn_dot(a, b):
    return lax.dot_general(a, b, (((1,), (0,)), ((), ())), preferred_element_type=jnp.float32)


def column_step(total):
    for step in (640, 512, 384, 256, 128):
        if total % step == 0:
            return step
    return total


def params(*semantics):
    return pltpu.CompilerParams(dimension_semantics=semantics, vmem_limit_bytes=VMEM_LIMIT)


def norm_project(x, gain, w_qkv):
    rows, width = x.shape
    cols = w_qkv.shape[1]
    step = column_step(cols)

    def body(x_ref, gain_ref, w_ref, out_ref, normed_ref):
        @pl.when(pl.program_id(0) == 0)
        def _():
            xf = x_ref[...].astype(jnp.float32)
            inv = lax.rsqrt(jnp.mean(xf * xf, axis=-1, keepdims=True) + eps)
            normed_ref[...] = (xf * inv * gain_ref[...]).astype(jnp.bfloat16)

        out_ref[...] = nn_dot(normed_ref[...], w_ref[...]).astype(jnp.bfloat16)

    return pl.pallas_call(
        body,
        grid=(cols // step,),
        in_specs=[
            pl.BlockSpec((rows, width), lambda n: (0, 0)),
            pl.BlockSpec((1, width), lambda n: (0, 0)),
            pl.BlockSpec((width, step), lambda n: (0, n)),
        ],
        out_specs=pl.BlockSpec((rows, step), lambda n: (0, n)),
        out_shape=jax.ShapeDtypeStruct((rows, cols), jnp.bfloat16),
        scratch_shapes=[pltpu.VMEM((rows, width), jnp.bfloat16)],
        compiler_params=params("arbitrary"),
        cost_estimate=pl.CostEstimate(
            flops=2 * rows * width * cols, bytes_accessed=2 * width * cols, transcendentals=0
        ),
        name="norm_project",
    )(x, gain, w_qkv)


def back_project(dy, w_out):
    rows, width = dy.shape
    step = 256

    def body(dy_ref, w_ref, out_ref):
        out_ref[...] = nt_dot(dy_ref[...], w_ref[...]).astype(jnp.bfloat16)

    return pl.pallas_call(
        body,
        grid=(width // step,),
        in_specs=[
            pl.BlockSpec((rows, width), lambda n: (0, 0)),
            pl.BlockSpec((step, width), lambda n: (n, 0)),
        ],
        out_specs=pl.BlockSpec((rows, step), lambda n: (0, n)),
        out_shape=jax.ShapeDtypeStruct((rows, width), jnp.bfloat16),
        compiler_params=params("arbitrary"),
        cost_estimate=pl.CostEstimate(
            flops=2 * rows * width * width, bytes_accessed=2 * width * width, transcendentals=0
        ),
        name="back_project",
    )(dy, w_out)


def head_window(head, width):
    tile = jnp.minimum(head * HD // LANES, width // LANES - 2)
    start = pl.multiple_of(tile * LANES, LANES)
    lane = lax.broadcasted_iota(jnp.int32, (1, 2 * LANES), 1) + start
    mask = jnp.logical_and(lane >= head * HD, lane < head * HD + HD)
    return start, mask


def query_side(qkv_blocks, d_context, key_bias):
    rows, width = d_context.shape
    blocks = len(qkv_blocks)
    scale = HD ** (-0.5)

    def body(*refs):
        qkv = refs[:blocks]
        dctx_ref, bias_ref, ctx_ref, dq_ref, stats_ref, stat_scratch = refs[blocks:]
        lane = lax.broadcasted_iota(jnp.int32, (1, LANES), 1)

        def head_step(head, _):
            start, mask = head_window(head, width)
            win = pl.ds(start, 2 * LANES)
            key_win = pl.ds(pl.multiple_of(start + width, LANES), 2 * LANES)
            value_win = pl.ds(pl.multiple_of(start + 2 * width, LANES), 2 * LANES)
            zero = jnp.zeros((), jnp.bfloat16)
            q = jnp.where(mask, qkv[0][:, win], zero)
            dc = jnp.where(mask, dctx_ref[:, win], zero)
            scores = [
                nt_dot(q, qkv[b][:, key_win]) * (scale * LOG2E)
                + bias_ref[:, b * rows : (b + 1) * rows]
                for b in range(blocks)
            ]
            top = functools.reduce(jnp.maximum, scores)
            top = jnp.max(top, axis=-1, keepdims=True)
            weights = [jnp.exp2(s - top) for s in scores]
            total = jnp.sum(functools.reduce(jnp.add, weights), axis=-1, keepdims=True)
            inv_total = 1.0 / total
            attn = [w * inv_total for w in weights]
            ctx = functools.reduce(
                jnp.add,
                [nn_dot(attn[b].astype(jnp.bfloat16), qkv[b][:, value_win]) for b in range(blocks)],
            )
            ctx_ref[:, win] = jnp.where(mask, ctx.astype(jnp.bfloat16), ctx_ref[:, win])
            d_attn = [nt_dot(dc, qkv[b][:, value_win]) for b in range(blocks)]
            inner = jnp.sum(
                functools.reduce(jnp.add, [attn[b] * d_attn[b] for b in range(blocks)]),
                axis=-1,
                keepdims=True,
            )
            d_scores = [(attn[b] * (d_attn[b] - inner)).astype(jnp.bfloat16) for b in range(blocks)]
            dq = functools.reduce(
                jnp.add, [nn_dot(d_scores[b], qkv[b][:, key_win]) for b in range(blocks)]
            )
            dq_ref[:, win] = jnp.where(mask, (dq * scale).astype(jnp.bfloat16), dq_ref[:, win])
            log_total = top + jnp.log2(total)
            stat = jnp.where(lane == head, log_total, stat_scratch[...])
            stat_scratch[...] = jnp.where(lane == head + H, inner, stat)
            return 0

        lax.fori_loop(0, H, head_step, 0)
        stats_ref[...] = jnp.transpose(stat_scratch[...])[: 2 * H]

    return pl.pallas_call(
        body,
        out_shape=(
            jax.ShapeDtypeStruct((rows, width), jnp.bfloat16),
            jax.ShapeDtypeStruct((rows, width), jnp.bfloat16),
            jax.ShapeDtypeStruct((2 * H, rows), jnp.float32),
        ),
        scratch_shapes=[pltpu.VMEM((rows, LANES), jnp.float32)],
        compiler_params=pltpu.CompilerParams(vmem_limit_bytes=VMEM_LIMIT),
        cost_estimate=pl.CostEstimate(
            flops=8 * H * rows * rows * blocks * 2 * LANES,
            bytes_accessed=6 * blocks * rows * width,
            transcendentals=0,
        ),
        name="query_side",
    )(*qkv_blocks, d_context, key_bias)


def key_side(qkv_blocks, dctx_blocks, stats_blocks, own_bias):
    rows, width = dctx_blocks[0].shape
    blocks = len(qkv_blocks)
    scale = HD ** (-0.5)

    def body(*refs):
        qkv = refs[:blocks]
        dctx = refs[blocks : 2 * blocks]
        stats = refs[2 * blocks : 3 * blocks]
        bias_ref, dk_ref, dv_ref = refs[3 * blocks :]

        def head_step(head, _):
            start, mask = head_window(head, width)
            win = pl.ds(start, 2 * LANES)
            key_win = pl.ds(pl.multiple_of(start + width, LANES), 2 * LANES)
            value_win = pl.ds(pl.multiple_of(start + 2 * width, LANES), 2 * LANES)
            zero = jnp.zeros((), jnp.bfloat16)
            k = jnp.where(mask, qkv[0][:, key_win], zero)
            v = jnp.where(mask, qkv[0][:, value_win], zero)
            dk = jnp.zeros((rows, 2 * LANES), jnp.float32)
            dv = jnp.zeros((rows, 2 * LANES), jnp.float32)
            for b in range(blocks):
                q = qkv[b][:, win]
                dc = dctx[b][:, win]
                log_total = stats[b][pl.ds(head, 1), :]
                inner = stats[b][pl.ds(head + H, 1), :]
                scores = nt_dot(k, q) * (scale * LOG2E) + bias_ref[...]
                attn = jnp.exp2(scores - log_total)
                dv = dv + nn_dot(attn.astype(jnp.bfloat16), dc)
                d_scores = attn * (nt_dot(v, dc) - inner)
                dk = dk + nn_dot(d_scores.astype(jnp.bfloat16), q)
            dk_ref[:, win] = jnp.where(mask, (dk * scale).astype(jnp.bfloat16), dk_ref[:, win])
            dv_ref[:, win] = jnp.where(mask, dv.astype(jnp.bfloat16), dv_ref[:, win])
            return 0

        lax.fori_loop(0, H, head_step, 0)

    return pl.pallas_call(
        body,
        out_shape=(
            jax.ShapeDtypeStruct((rows, width), jnp.bfloat16),
            jax.ShapeDtypeStruct((rows, width), jnp.bfloat16),
        ),
        compiler_params=pltpu.CompilerParams(vmem_limit_bytes=VMEM_LIMIT),
        cost_estimate=pl.CostEstimate(
            flops=8 * H * rows * rows * blocks * 2 * LANES,
            bytes_accessed=6 * blocks * rows * width,
            transcendentals=0,
        ),
        name="key_side",
    )(*qkv_blocks, *dctx_blocks, *stats_blocks, own_bias)


def project_out(x, context, w_out):
    rows, width = x.shape
    step = 256

    def body(x_ref, ctx_ref, w_ref, out_ref):
        out_ref[...] = (
            x_ref[...].astype(jnp.float32) + nn_dot(ctx_ref[...], w_ref[...])
        ).astype(jnp.bfloat16)

    return pl.pallas_call(
        body,
        grid=(width // step,),
        in_specs=[
            pl.BlockSpec((rows, step), lambda n: (0, n)),
            pl.BlockSpec((rows, width), lambda n: (0, 0)),
            pl.BlockSpec((width, step), lambda n: (0, n)),
        ],
        out_specs=pl.BlockSpec((rows, step), lambda n: (0, n)),
        out_shape=jax.ShapeDtypeStruct((rows, width), jnp.bfloat16),
        compiler_params=params("arbitrary"),
        cost_estimate=pl.CostEstimate(
            flops=2 * rows * width * width, bytes_accessed=2 * width * width, transcendentals=0
        ),
        name="project_out",
    )(x, context, w_out)


def input_gradient(x, dy, gain, dq, dk, dv, w_qkv):
    rows, width = x.shape
    step = width // 2
    halves = width // step

    def body(x_ref, dy_ref, gain_ref, dq_ref, dk_ref, dv_ref, w_ref, out_ref, acc_ref):
        n = pl.program_id(0)

        @pl.when(n == 0)
        def _():
            acc_ref[...] = nt_dot(dq_ref[...], w_ref[...])

        @pl.when(jnp.logical_and(n > 0, n < halves))
        def _():
            acc_ref[...] += nt_dot(dq_ref[...], w_ref[...])

        @pl.when(jnp.logical_and(n >= halves, n < 2 * halves))
        def _():
            acc_ref[...] += nt_dot(dk_ref[...], w_ref[...])

        @pl.when(n >= 2 * halves)
        def _():
            acc_ref[...] += nt_dot(dv_ref[...], w_ref[...])

        @pl.when(n == 3 * halves - 1)
        def _():
            xf = x_ref[...].astype(jnp.float32)
            inv = lax.rsqrt(jnp.mean(xf * xf, axis=-1, keepdims=True) + eps)
            scaled = gain_ref[...] * acc_ref[...]
            along = jnp.mean(xf * scaled, axis=-1, keepdims=True)
            grad = dy_ref[...].astype(jnp.float32) + inv * scaled - xf * (inv * inv * inv) * along
            out_ref[...] = grad.astype(jnp.bfloat16)

    whole = pl.BlockSpec((rows, width), lambda n: (0, 0))

    def piece(first):
        return pl.BlockSpec(
            (rows, step), lambda n: (0, jnp.clip(n - first * halves, 0, halves - 1))
        )

    return pl.pallas_call(
        body,
        grid=(3 * halves,),
        in_specs=[
            whole,
            whole,
            pl.BlockSpec((1, width), lambda n: (0, 0)),
            piece(0),
            piece(1),
            piece(2),
            pl.BlockSpec((width, step), lambda n: (0, n)),
        ],
        out_specs=whole,
        out_shape=jax.ShapeDtypeStruct((rows, width), jnp.bfloat16),
        scratch_shapes=[pltpu.VMEM((rows, width), jnp.float32)],
        compiler_params=params("arbitrary"),
        cost_estimate=pl.CostEstimate(
            flops=6 * rows * width * width, bytes_accessed=6 * width * width, transcendentals=0
        ),
        name="input_gradient",
    )(x, dy, gain, dq, dk, dv, w_qkv)


def shards(names, patches, cotangent, counts, gain, w_qkv, w_out):
    home, width = patches.shape
    members = lax.axis_size("k")
    devices = lax.axis_size(names)
    cap = 2 * home // devices
    outer = lax.axis_size("o")
    inner = lax.axis_size("j")
    own = lax.axis_index(names)
    group = lax.axis_index("o") * inner + lax.axis_index("j")
    member = lax.axis_index("k")
    gain_row = gain.reshape(1, width)

    plan = counts.reshape(devices, devices)
    plan_row = lax.dynamic_index_in_dim(plan, own, 0, keepdims=False)
    order = jnp.arange(devices, dtype=jnp.int32)
    offsets = jnp.sum(jnp.where(order[None, :] < order[:, None], plan_row[None, :], 0), axis=1)
    slots = jnp.arange(cap, dtype=jnp.int32)
    row_of_slot = jnp.where(slots[None, :] < plan_row[:, None], offsets[:, None] + slots[None, :], -1)
    if names == ("o", "k", "j"):
        row_of_slot = row_of_slot.reshape(outer, inner, members, cap).transpose(0, 2, 1, 3)
    row_of_slot = row_of_slot.reshape(devices * cap)
    place = (
        row_of_slot[:, None] == jnp.arange(home, dtype=jnp.int32)[None, :]
    ).astype(jnp.bfloat16)

    def pack(values):
        return nn_dot(place, values).astype(jnp.bfloat16)

    def unpack(values):
        return lax.dot_general(
            place, values, (((0,), (0,)), ((), ())), preferred_element_type=jnp.float32
        ).astype(jnp.bfloat16)

    def route(values):
        shaped = values.reshape(devices, cap, width)
        moved = lax.all_to_all(shaped, names, split_axis=0, concat_axis=0, tiled=True)
        return moved.reshape(devices * cap, width)

    def swap(values, bits):
        pairs = [(m, m ^ bits) for m in range(members)]
        return lax.ppermute(values, "k", pairs)

    def collect(values):
        held = {0: values}
        bit = members // 2
        while bit:
            for place_held in sorted(held, reverse=True):
                held[place_held ^ bit] = swap(held[place_held], bit)
            bit //= 2
        return [held[b] for b in range(members)]

    x = route(pack(patches))
    dy = route(pack(cotangent))
    x_blocks = collect(x)
    dy_blocks = collect(dy)

    incoming = lax.dynamic_index_in_dim(
        counts.reshape(devices, outer * inner, members), group, 1, keepdims=False
    )
    partner = jnp.arange(members, dtype=jnp.int32) ^ member
    arrivals = jnp.take(incoming, partner, axis=1).T
    live = slots[None, None, :] < arrivals[:, :, None]
    bias = jnp.where(live, 0.0, DEAD).reshape(members, devices * cap)

    qkv_blocks = [norm_project(block, gain_row, w_qkv) for block in x_blocks]
    dctx_blocks = [back_project(block, w_out) for block in dy_blocks]
    context, dq, stats = query_side(qkv_blocks, dctx_blocks[0], bias.reshape(1, -1))
    output = project_out(x, context, w_out)
    back_out = route(output)
    stats_blocks = [stats] + [swap(stats, b) for b in range(1, members)]
    dk, dv = key_side(qkv_blocks, dctx_blocks, stats_blocks, bias[0].reshape(-1, 1))
    grad = input_gradient(x, dy, gain_row, dq, dk, dv, w_qkv)
    back_grad = route(grad)
    return unpack(back_out), unpack(back_grad)


def solution(mesh):
    dp = mesh.shape["dp"]
    enc = mesh.shape["enc"]
    if dp % enc == 0:
        names, sizes = ("o", "k", "j"), (dp // enc, enc, enc)
    else:
        names, sizes = ("o", "j", "k"), (dp, 1, enc)
    fine = Mesh(mesh.devices.reshape(sizes), names)
    return jax.shard_map(
        functools.partial(shards, names),
        mesh=fine,
        in_specs=(P(names, None), P(names, None), P(), P(), P(), P()),
        out_specs=(P(names, None), P(names, None)),
        check_vma=False,
    )
```

time: 465 us -> 212 us (0.46)
  matrix products: 188 us -> 4.67 us
  Pallas kernels: 0 us -> 120 us
  waiting for transfers between devices: 159 us -> 50.5 us
  local copies, waits for them, and re-layouts: 34 us -> 7.46 us
  blocking collectives: 24.9 us -> 0 us
  other arithmetic: 24.6 us -> 0.38 us
  between operations: 14.2 us -> 0.82 us
  starting transfers between devices: 15 us -> 26.6 us
    dot_general x101 -> x4, matrix products: 188 us -> 4.67 us  [the longest x2 2.48 us: nn_dot(): lax.dot_general(a, b, (((1,), (0,)), ((), ())), preferred_element_type=jn...]
    pallas_call x0 -> x12, Pallas kernels: none -> 120 us  [the longest x4 35.2 us: norm_project(): pl.pallas_call(body, grid=(cols // step,), in_specs=[pl.BlockSpec((rows,...]
    reduce_scatter x1 -> x0, waiting for transfers between devices: 96.1 us -> none  [shards(): lax.psum_scatter(d_kv.astype(jnp.bfloat16), 'enc', scatter_dimension=0, t...]
    all_to_all x1 -> x0, blocking collectives: 24.9 us -> none  [shards(): lax.all_to_all(packed_x, ('dp', 'enc'), split_axis=0, concat_axis=0, tile...]
    all_gather x1 -> x0, waiting for transfers between devices: 22.9 us -> none  [shards(): all_normed = lax.all_gather(normed, 'enc', axis=0, tiled=True)]
    gather x4 -> x1, local copies, waits for them, and re-layouts: 13.4 us -> 0.57 us  [shards(): arrivals = jnp.take(incoming, partner, axis=1).T]
    slice x3 -> x1, local copies, waits for them, and re-layouts: 11.6 us -> 0.01 us  [shards(): bias[0].reshape(-1, 1)]
    all_to_all x3 -> x4, waiting for transfers between devices: 39.7 us -> 49.6 us  [route(): lax.all_to_all(shaped, names, split_axis=0, concat_axis=0, tiled=True)]
  transfers between devices with their start and end apart: 5 -> 13, of which waited for: 4 -> 4; matrix products, arithmetic and copies ran while one was open for 6% -> 3% of each run, Pallas kernels for 0% -> 57%
where the time goes in v1:
time: 212 us; the launch traced here: 210 us
  Pallas kernels  120 us (57%)
  waiting for transfers between devices  50.5 us (24%)
  starting transfers between devices  26.6 us (13%)
  local copies, waits for them, and re-layouts  7.46 us (4%)
  matrix products  4.67 us (2%)
    all_to_all x4, waiting for transfers between devices, route(): lax.all_to_all(shaped, names, split_axis=0, concat_axis=0, tiled=True)  49.6 us
    pallas_call x4, Pallas kernels, norm_project(): pl.pallas_call(body, grid=(cols // step,), in_specs=[pl.BlockSpec((rows,...  35.2 us
    pallas_call x1, Pallas kernels, query_side(): pl.pallas_call(body, out_shape=(jax.ShapeDtypeStruct((rows, width), jnp.b...  27.2 us
    pallas_call x4, Pallas kernels, back_project(): pl.pallas_call(body, grid=(width // step,), in_specs=[pl.BlockSpec((rows,...  21.6 us
    pallas_call x1, Pallas kernels, key_side(): pl.pallas_call(body, out_shape=(jax.ShapeDtypeStruct((rows, width), jnp.b...  20.5 us
    all_to_all x4, starting transfers between devices, route(): lax.all_to_all(shaped, names, split_axis=0, concat_axis=0, tiled=True)  20.3 us
    pallas_call x1, Pallas kernels, input_gradient(): pl.pallas_call(body, grid=(3 * halves,), in_specs=[whole, whole, pl.Block...  9.88 us
    ppermute x9, starting transfers between devices, swap(): return lax.ppermute(values, 'k', pairs)  6.32 us
  transfers between devices with their start and end apart: 13, of which 4 were waited for; matrix products, arithmetic and copies ran while one was open for 3% of the time, Pallas kernels for 57%

profile of v1, /device:TPU:1, one launch (start us, length us, event | category | flops | bytes accessed | tf_op | source)
XLA Modules:
  0.0 210.4 jit_solution(4685978577874457402)
XLA Ops:
  0.7 1.2 copy.16
  2.7 1.3 fusion
  3.9 7.1 %all-to-all-start = ((bf16[32,8,1280]{2,1,0:T(8,128)(2,1)}), bf16[32,8,1280]{2,1,0:T(8,128)(2,1)S(1)}, u32[]{:S(2)}, u32[]{:S(2)}) async-start(bf16[32,8,1280]{2,1,0:T(8,128)(2,1)} %fusion), calls=%async_computation | async-start | bytes 1310720 | tf_op jit(solution)/shard_map/all_to_all | solution.py:353
  11.0 1.2 fusion.1
  12.2 16.8 %all-to-all-done = bf16[32,8,1280]{2,1,0:T(8,128)(2,1)S(1)} async-done(((bf16[32,8,1280]{2,1,0:T(8,128)(2,1)}), bf16[32,8,1280]{2,1,0:T(8,128)(2,1)S(1)}, u32[]{:S(2)}, u32[]{:S(2)}) %all-to-all-start) | async-done | bytes 655392 | tf_op jit(solution)/shard_map/all_to_all | solution.py:353
  29.0 3.2 %all-to-all-start.1 = ((bf16[32,8,1280]{2,1,0:T(8,128)(2,1)}), bf16[32,8,1280]{2,1,0:T(8,128)(2,1)S(1)}, u32[]{:S(2)}, u32[]{:S(2)}) async-start(bf16[32,8,1280]{2,1,0:T(8,128)(2,1)} %fusion.1), calls=%async_computation.1 | async-start | bytes 1310720 | tf_op jit(solution)/shard_map/all_to_all | solution.py:353
  32.3 1.4 collective-permute-start.1
  34.4 15.9 %all-to-all-done.1 = bf16[32,8,1280]{2,1,0:T(8,128)(2,1)S(1)} async-done(((bf16[32,8,1280]{2,1,0:T(8,128)(2,1)}), bf16[32,8,1280]{2,1,0:T(8,128)(2,1)S(1)}, u32[]{:S(2)}, u32[]{:S(2)}) %all-to-all-start.1) | async-done | bytes 655392 | tf_op jit(solution)/shard_map/all_to_all | solution.py:353
  50.3 1.2 collective-permute-start.4
  53.0 0.8 reshape_squeeze.4.refs_12_
  54.2 5.4 %back_project.4.refs_4_ = bf16[256,1280]{1,0:T(8,128)(2,1)} custom-call(bf16[256,1280]{1,0:T(8,128)(2,1)} %bitcast.34, bf16[1280,1280]{1,0:T(8,128)(2,1)} %w_ref.18), custom_call_target="tpu_custom_call" | custom-call | flops 838860800 | bytes 3276800 | tf_op jit(solution)/shard_map/back_project/pallas_call | solution.py:79
  59.8 8.9 %norm_project.4.refs_0_ = bf16[256,3840]{1,0:T(8,128)(2,1)} custom-call(bf16[256,1280]{1,0:T(8,128)(2,1)} %bitcast.28, f32[1,1280]{1,0:T(1,128)} %reshape.122.gain_ref, bf16[1280,3840]{1,0:T(8,128)(2,1)} %w_ref.19), custom_call_target="tpu_custom_call" | custom-call | flops 2516582400 | bytes 9830400 | tf_op jit(solution)/shard_map/norm_project/pallas_call | solution.py:53
  68.7 0.9 collective-permute-done.4.dy_ref
  69.5 1.0 collective-permute-start.5
  70.5 8.8 %norm_project.6.refs_2_ = bf16[256,3840]{1,0:T(8,128)(2,1)} custom-call(bf16[256,1280]{1,0:T(8,128)(2,1)} %copy-done.3, f32[1,1280]{1,0:T(1,128)} %reshape.122.gain_ref, bf16[1280,3840]{1,0:T(8,128)(2,1)} %w_ref.19), custom_call_target="tpu_custom_call" | custom-call | flops 2516582400 | bytes 9830400 | tf_op jit(solution)/shard_map/norm_project/pallas_call | solution.py:53
  79.3 0.8 copy-done.4
  80.1 8.8 %norm_project.5.refs_1_ = bf16[256,3840]{1,0:T(8,128)(2,1)} custom-call(bf16[256,1280]{1,0:T(8,128)(2,1)} %copy-done.4, f32[1,1280]{1,0:T(1,128)} %reshape.122.gain_ref, bf16[1280,3840]{1,0:T(8,128)(2,1)} %w_ref.19), custom_call_target="tpu_custom_call" | custom-call | flops 2516582400 | bytes 9830400 | tf_op jit(solution)/shard_map/norm_project/pallas_call | solution.py:53
  88.9 0.8 copy-done.5
  89.7 8.8 %norm_project.7.refs_3_ = bf16[256,3840]{1,0:T(8,128)(2,1)} custom-call(bf16[256,1280]{1,0:T(8,128)(2,1)} %copy-done.5, f32[1,1280]{1,0:T(1,128)} %reshape.122.gain_ref, bf16[1280,3840]{1,0:T(8,128)(2,1)} %w_ref.19), custom_call_target="tpu_custom_call" | custom-call | flops 2516582400 | bytes 9830400 | tf_op jit(solution)/shard_map/norm_project/pallas_call | solution.py:53
  98.5 27.2 %query_side.1 = (bf16[256,1280]{1,0:T(8,128)(2,1)}, bf16[256,1280]{1,0:T(8,128)(2,1)}, f32[32,256]{1,0:T(8,128)}) custom-call(bf16[256,3840]{1,0:T(8,128)(2,1)} %norm_project.4.refs_0_, bf16[256,3840]{1,0:T(8,128)(2,1)} %norm_project.5.refs_1_, bf16[256,3840]{1,0:T(8,128)(2,1)} %norm_project.6.refs_2_, bf16[256,3840]{1,0:T(8,128)(2,1)} %norm_project.7.refs_3_, ...), custom_call_target="tpu_custom_call" | custom-call | flops 8589934592 | bytes 7864320 | tf_op jit(solution)/shard_map/query_side/pallas_call | solution.py:157
  125.6 5.6 %project_out.1 = bf16[256,1280]{1,0:T(8,128)(2,1)} custom-call(bf16[256,1280]{1,0:T(8,128)(2,1)} %bitcast.29, bf16[256,1280]{1,0:T(8,128)(2,1)} %get-tuple-element.7.ctx_ref, bf16[1280,1280]{1,0:T(8,128)(2,1)} %w_ref.18), custom_call_target="tpu_custom_call" | custom-call | flops 838860800 | bytes 3276800 | tf_op jit(solution)/shard_map/project_out/pallas_call | solution.py:237
  131.2 4.5 %all-to-all-start.2 = ((bf16[32,8,1280]{2,1,0:T(8,128)(2,1)}), bf16[32,8,1280]{2,1,0:T(8,128)(2,1)S(1)}, u32[]{:S(2)}, u32[]{:S(2)}) async-start(bf16[32,8,1280]{2,1,0:T(8,128)(2,1)} %bitcast.37), calls=%async_computation.2 | async-start | bytes 1310720 | tf_op jit(solution)/shard_map/all_to_all | solution.py:353
  135.7 5.4 %back_project.6.refs_6_ = bf16[256,1280]{1,0:T(8,128)(2,1)} custom-call(bf16[256,1280]{1,0:T(8,128)(2,1)} %collective-permute-done.4.dy_ref, bf16[1280,1280]{1,0:T(8,128)(2,1)} %w_ref.18), custom_call_target="tpu_custom_call" | custom-call | flops 838860800 | bytes 3276800 | tf_op jit(solution)/shard_map/back_project/pallas_call | solution.py:79
  141.1 5.4 %back_project.5.refs_5_ = bf16[256,1280]{1,0:T(8,128)(2,1)} custom-call(bf16[256,1280]{1,0:T(8,128)(2,1)} %collective-permute-done.3.dy_ref, bf16[1280,1280]{1,0:T(8,128)(2,1)} %w_ref.18), custom_call_target="tpu_custom_call" | custom-call | flops 838860800 | bytes 3276800 | tf_op jit(solution)/shard_map/back_project/pallas_call | solution.py:79
  146.6 1.6 collective-permute-start.8
  148.7 5.4 %back_project.7.refs_7_ = bf16[256,1280]{1,0:T(8,128)(2,1)} custom-call(bf16[256,1280]{1,0:T(8,128)(2,1)} %collective-permute-done.5.dy_ref, bf16[1280,1280]{1,0:T(8,128)(2,1)} %w_ref.18), custom_call_target="tpu_custom_call" | custom-call | flops 838860800 | bytes 3276800 | tf_op jit(solution)/shard_map/back_project/pallas_call | solution.py:79
  155.3 20.5 %key_side.1 = (bf16[256,1280]{1,0:T(8,128)(2,1)}, bf16[256,1280]{1,0:T(8,128)(2,1)}) custom-call(bf16[256,3840]{1,0:T(8,128)(2,1)} %norm_project.4.refs_0_, bf16[256,3840]{1,0:T(8,128)(2,1)} %norm_project.5.refs_1_, bf16[256,3840]{1,0:T(8,128)(2,1)} %norm_project.6.refs_2_, bf16[256,3840]{1,0:T(8,128)(2,1)} %norm_project.7.refs_3_, ...), custom_call_target="tpu_custom_call" | custom-call | flops 8589934592 | bytes 7864320 | tf_op jit(solution)/shard_map/key_side/pallas_call | solution.py:212
  175.8 9.9 %input_gradient.1 = bf16[256,1280]{1,0:T(8,128)(2,1)} custom-call(bf16[256,1280]{1,0:T(8,128)(2,1)} %bitcast.30, bf16[256,1280]{1,0:T(8,128)(2,1)} %bitcast.35, f32[1,1280]{1,0:T(1,128)} %reshape.122.gain_ref, bf16[256,1280]{1,0:T(8,128)(2,1)} %get-tuple-element.8.dq_ref, bf16[256,1280]{1,0:T(8,128)(2,1)} %get-tuple-element.10.dk_ref, ...), custom_call_target="tpu_custom_call" | custom-call | flops 2516582400 | bytes 9830400 | tf_op jit(solution)/shard_map/input_gradient/pallas_call | solution.py:295
  185.7 5.6 %all-to-all-start.3 = ((bf16[32,8,1280]{2,1,0:T(8,128)(2,1)}), bf16[32,8,1280]{2,1,0:T(8,128)(2,1)S(1)}, u32[]{:S(2)}, u32[]{:S(2)}) async-start(bf16[32,8,1280]{2,1,0:T(8,128)(2,1)} %bitcast.36), calls=%async_computation.3 | async-start | bytes 1310720 | tf_op jit(solution)/shard_map/all_to_all | solution.py:353
  191.3 1.1 convolution_convert_fusion.3
  192.4 16.9 %all-to-all-done.3 = bf16[32,8,1280]{2,1,0:T(8,128)(2,1)S(1)} async-done(((bf16[32,8,1280]{2,1,0:T(8,128)(2,1)}), bf16[32,8,1280]{2,1,0:T(8,128)(2,1)S(1)}, u32[]{:S(2)}, u32[]{:S(2)}) %all-to-all-start.3) | async-done | bytes 655392 | tf_op jit(solution)/shard_map/all_to_all | solution.py:353
  209.3 1.1 convolution_convert_fusion.2
  (58 shorter events, 5.4 us)
Async XLA Ops:
  0.6 2.0 copy-start
  0.6 10.4 %copy-start.6 = (bf16[128,1280]{1,0:T(8,128)(2,1)S(1)}, bf16[128,1280]{1,0:T(8,128)(2,1)}, u32[]{:S(2)}) copy-start(bf16[128,1280]{1,0:T(8,128)(2,1)} %param.7) | copy-start | bytes 983044
  3.9 28.3 %copy-start.7 = (s32[8,4,8,4]{2,3,1,0:T(4,128)S(1)}, s32[8,4,8,4]{2,3,1,0:T(4,128)}, u32[]{:S(2)}) copy-start(s32[8,4,8,4]{2,3,1,0:T(4,128)} %param.8) | copy-start | bytes 12292
  3.9 48.5 %copy-start.8 = (f32[1280]{0:T(1024)S(1)}, f32[1280]{0:T(1024)}, u32[]{:S(2)}) copy-start(f32[1280]{0:T(1024)} %param.9) | copy-start | bytes 15364
  3.9 25.1 %all-to-all-start = ((bf16[32,8,1280]{2,1,0:T(8,128)(2,1)}), bf16[32,8,1280]{2,1,0:T(8,128)(2,1)S(1)}, u32[]{:S(2)}, u32[]{:S(2)}) async-start(bf16[32,8,1280]{2,1,0:T(8,128)(2,1)} %fusion), calls=%async_computation | async-start | bytes 1310720 | tf_op jit(solution)/shard_map/all_to_all | solution.py:353
  29.0 30.6 %copy-start.1 = (bf16[32,8,1280]{2,1,0:T(8,128)(2,1)}, bf16[32,8,1280]{2,1,0:T(8,128)(2,1)S(1)}, u32[]{:S(2)}) copy-start(bf16[32,8,1280]{2,1,0:T(8,128)(2,1)S(1)} %all-to-all-done) | copy-start | bytes 1966084
  29.0 21.3 %all-to-all-start.1 = ((bf16[32,8,1280]{2,1,0:T(8,128)(2,1)}), bf16[32,8,1280]{2,1,0:T(8,128)(2,1)S(1)}, u32[]{:S(2)}, u32[]{:S(2)}) async-start(bf16[32,8,1280]{2,1,0:T(8,128)(2,1)} %fusion.1), calls=%async_computation.1 | async-start | bytes 1310720 | tf_op jit(solution)/shard_map/all_to_all | solution.py:353
  32.3 27.3 %collective-permute-start.1 = (bf16[256,1280]{1,0:T(8,128)(2,1)S(1)}, bf16[256,1280]{1,0:T(8,128)(2,1)S(1)}, u32[]{:S(2)}, u32[]{:S(2)}) collective-permute-start(bf16[256,1280]{1,0:T(8,128)(2,1)S(1)} %bitcast.26), channel_id=1, source_target_pairs={{0,8},{4,12},{8,0},{12,4},{1,9},{5,13},{9,1},{13,5},{2,10},{6,14},... | collective-permute-start | bytes 1966088 | tf_op jit(solution)/shard_map/ppermute | solution.py:358
  50.3 3.9 %copy-start.2 = (bf16[32,8,1280]{2,1,0:T(8,128)(2,1)}, bf16[32,8,1280]{2,1,0:T(8,128)(2,1)S(1)}, u32[]{:S(2)}) copy-start(bf16[32,8,1280]{2,1,0:T(8,128)(2,1)S(1)} %all-to-all-done.1) | copy-start | bytes 1966084
  50.3 19.2 %collective-permute-start.4 = (bf16[256,1280]{1,0:T(8,128)(2,1)S(1)}, bf16[256,1280]{1,0:T(8,128)(2,1)}, u32[]{:S(2)}, u32[]{:S(2)}) collective-permute-start(bf16[256,1280]{1,0:T(8,128)(2,1)S(1)} %bitcast.32), channel_id=1, source_target_pairs={{0,8},{4,12},{8,0},{12,4},{1,9},{5,13},{9,1},{13,5},{2,10},{6,14},... | collective-permute-start | bytes 1966088 | tf_op jit(solution)/shard_map/ppermute | solution.py:358
  51.6 27.7 %collective-permute-start = (bf16[256,1280]{1,0:T(8,128)(2,1)S(1)}, bf16[256,1280]{1,0:T(8,128)(2,1)S(1)}, u32[]{:S(2)}, u32[]{:S(2)}) collective-permute-start(bf16[256,1280]{1,0:T(8,128)(2,1)S(1)} %bitcast.27), channel_id=1, source_target_pairs={{0,4},{4,0},{8,12},{12,8},{1,5},{5,1},{9,13},{13,9},{2,6},{6,2},{1... | collective-permute-start | bytes 1966088 | tf_op jit(solution)/shard_map/ppermute | solution.py:358
  53.7 87.4 %collective-permute-start.3 = (bf16[256,1280]{1,0:T(8,128)(2,1)S(1)}, bf16[256,1280]{1,0:T(8,128)(2,1)}, u32[]{:S(2)}, u32[]{:S(2)}) collective-permute-start(bf16[256,1280]{1,0:T(8,128)(2,1)S(1)} %bitcast.33), channel_id=1, source_target_pairs={{0,4},{4,0},{8,12},{12,8},{1,5},{5,1},{9,13},{13,9},{2,6},{6,2},{1... | collective-permute-start | bytes 1966088 | tf_op jit(solution)/shard_map/ppermute | solution.py:358
  59.7 9.0 %copy-start.3 = (bf16[256,1280]{1,0:T(8,128)(2,1)}, bf16[256,1280]{1,0:T(8,128)(2,1)S(1)}, u32[]{:S(2)}) copy-start(bf16[256,1280]{1,0:T(8,128)(2,1)S(1)} %collective-permute-done.1.x_ref) | copy-start | bytes 1966084
  59.7 29.2 %collective-permute-start.2 = (bf16[256,1280]{1,0:T(8,128)(2,1)S(1)}, bf16[256,1280]{1,0:T(8,128)(2,1)S(1)}, u32[]{:S(2)}, u32[]{:S(2)}) collective-permute-start(bf16[256,1280]{1,0:T(8,128)(2,1)S(1)} %collective-permute-done.1.x_ref), channel_id=1, source_target_pairs={{0,4},{4,0},{8,12},{12,8},{1,5},{5,1},{9,13},{13,9},{2,6},{6,2},{1... | collective-permute-start | bytes 1966088 | tf_op jit(solution)/shard_map/ppermute | solution.py:358
  69.5 79.2 %collective-permute-start.5 = (bf16[256,1280]{1,0:T(8,128)(2,1)}, bf16[256,1280]{1,0:T(8,128)(2,1)}, u32[]{:S(2)}, u32[]{:S(2)}) collective-permute-start(bf16[256,1280]{1,0:T(8,128)(2,1)} %collective-permute-done.4.dy_ref), channel_id=1, source_target_pairs={{0,4},{4,0},{8,12},{12,8},{1,5},{5,1},{9,13},{13,9},{2,6},{6,2},{1... | collective-permute-start | bytes 1966088 | tf_op jit(solution)/shard_map/ppermute | solution.py:358
  79.3 0.8 copy-start.4
  88.9 0.8 copy-start.5
  131.2 54.5 %all-to-all-start.2 = ((bf16[32,8,1280]{2,1,0:T(8,128)(2,1)}), bf16[32,8,1280]{2,1,0:T(8,128)(2,1)S(1)}, u32[]{:S(2)}, u32[]{:S(2)}) async-start(bf16[32,8,1280]{2,1,0:T(8,128)(2,1)} %bitcast.37), calls=%async_computation.2 | async-start | bytes 1310720 | tf_op jit(solution)/shard_map/all_to_all | solution.py:353
  141.1 5.4 %copy-start.9 = (f32[32,256]{1,0:T(8,128)S(1)}, f32[32,256]{1,0:T(8,128)}, u32[]{:S(2)}) copy-start(f32[32,256]{1,0:T(8,128)} %get-tuple-element.9.refs_8_) | copy-start | bytes 98308
  146.6 7.5 %collective-permute-start.8 = (f32[32,256]{1,0:T(8,128)S(1)}, f32[32,256]{1,0:T(8,128)S(1)}, u32[]{:S(2)}, u32[]{:S(2)}) collective-permute-start(f32[32,256]{1,0:T(8,128)S(1)} %copy-done.9), channel_id=1, source_target_pairs={{0,12},{4,8},{8,4},{12,0},{1,13},{5,9},{9,5},{13,1},{2,14},{6,10},... | collective-permute-start | bytes 98312 | tf_op jit(solution)/shard_map/ppermute | solution.py:358
  148.2 5.9 %collective-permute-start.7 = (f32[32,256]{1,0:T(8,128)S(1)}, f32[32,256]{1,0:T(8,128)S(1)}, u32[]{:S(2)}, u32[]{:S(2)}) collective-permute-start(f32[32,256]{1,0:T(8,128)S(1)} %copy-done.9), channel_id=1, source_target_pairs={{0,8},{4,12},{8,0},{12,4},{1,9},{5,13},{9,1},{13,5},{2,10},{6,14},... | collective-permute-start | bytes 98312 | tf_op jit(solution)/shard_map/ppermute | solution.py:358
  148.2 5.9 %collective-permute-start.6 = (f32[32,256]{1,0:T(8,128)S(1)}, f32[32,256]{1,0:T(8,128)S(1)}, u32[]{:S(2)}, u32[]{:S(2)}) collective-permute-start(f32[32,256]{1,0:T(8,128)S(1)} %copy-done.9), channel_id=1, source_target_pairs={{0,4},{4,0},{8,12},{12,8},{1,5},{5,1},{9,13},{13,9},{2,6},{6,2},{1... | collective-permute-start | bytes 98312 | tf_op jit(solution)/shard_map/ppermute | solution.py:358
  154.1 0.6 copy-start.10
  154.1 0.6 copy-start.11
  154.7 0.6 copy-start.12
  185.7 23.6 %all-to-all-start.3 = ((bf16[32,8,1280]{2,1,0:T(8,128)(2,1)}), bf16[32,8,1280]{2,1,0:T(8,128)(2,1)S(1)}, u32[]{:S(2)}, u32[]{:S(2)}) async-start(bf16[32,8,1280]{2,1,0:T(8,128)(2,1)} %bitcast.36), calls=%async_computation.3 | async-start | bytes 1310720 | tf_op jit(solution)/shard_map/all_to_all | solution.py:353
